TPU v7x, 32 devices: a whole 2x2x4 slice. The times are simulated.
32 devices in a mesh: groups: 2 (over y), seq: 4 (over z), head: 2 (over x), rep: 2 (over core).
Axes of the slice: x: 2, y: 2, z: 4, core: 2. Of those that a mesh axis runs over, the one named last changes fastest.
Arguments:
- queries: bfloat16 [128, 64, 128], P(('groups', 'seq', 'rep'), 'head'), parts along dimension 0, may hold values from -256 to 256
- page_owner: int32 [128, 128], P(('groups', 'seq', 'rep')), parts along dimension 0, may hold values from -1 to 3, as said below
- page_slot: int32 [128, 128], P(('groups', 'seq', 'rep')), parts along dimension 0, may hold values from -1 to 63, as said below
- lengths: int32 [128], P(('groups', 'seq', 'rep')), parts along dimension 0, may hold values from 1 to 16384, as said below
- keys: bfloat16 [1024, 8, 128, 128], P(('groups', 'seq', 'rep'), 'head'), parts along dimension 0, may hold values from -24 to 24
- values: bfloat16 [1024, 8, 128, 128], P(('groups', 'seq', 'rep'), 'head'), parts along dimension 0, may hold values from -6 to 6
Outputs:
- attended: bfloat16 [128, 64, 128], P(('groups', 'seq', 'rep'), 'head'), parts along dimension 0
There are 2 independent parts, one for each index of `groups`. A program takes and returns all parts, laid end to end along the dimension named above; each array names one. Nothing has to cross between parts.
Inputs may be any that keep to these rules, and one draw needn't show every extreme that they name: `page_owner`: for j below ceil(lengths[r] / 128) the seq index of the device, among those of r's half (r // 8) % 2, whose pool holds page j of r; -1 for later j. `page_slot`: the page's slot in that pool, -1 where page_owner is -1. No slot of a pool holds two pages; in each half, some device's pool has all 64 slots in use. `lengths`: in each half some request has the most.
All inputs are finite; a program needn't handle non-finite values.
Results may differ from a plain program's by a relative error of at most 0.0041.
Values may be sent and summed in bfloat16 or wider, within the bound.
A program may use at most 64 MiB of HBM per device.

v0:
```python
import functools
import math

import jax
import jax.numpy as jnp
from jax import lax
from jax.experimental import pallas as pl
from jax.experimental.pallas import tpu as pltpu
from jax.sharding import PartitionSpec as P

MASKED = -1e30
F32 = jnp.float32
BF16 = jnp.bfloat16
NT = (((1,), (1,)), ((), ()))


def iota(shape, dim):
    return lax.broadcasted_iota(jnp.int32, shape, dim)


def kernel(
    n, unroll, lens_ref, q_ref, owner_ref, slot_ref, k_hbm, v_hbm, out_ref,
    kbuf, vbuf, qall, tsend, trecv, liveb, reqb, mt, m, qslot, pmb, lb, wbuf, ohi,
    osend, orecv, ssend, srecv,
    ksem, vsem, tss, trs, qss, qrs, oss, ors, sss, srs,
):
    pool, kv, tokens, width = k_hbm.shape
    rows = q_ref.shape[0]
    group = q_ref.shape[1] // kv
    block = rows * group
    lanes = trecv.shape[2]
    scale = 1.0 / math.sqrt(width)
    me = lax.axis_index("seq")

    def peer(off):
        return {"seq": lax.rem(me + off, n)}

    def source(off):
        return {"seq": lax.rem(me + n - off, n)}

    def remote(src, dst, ssem, rsem, to):
        return pltpu.make_async_remote_copy(
            src_ref=src, dst_ref=dst, send_sem=ssem, recv_sem=rsem,
            device_id=to, device_id_type=pl.DeviceIdType.MESH,
        )

    barrier = pltpu.get_barrier_semaphore()
    for off in range(1, n):
        pl.semaphore_signal(
            barrier, inc=1, device_id=peer(off), device_id_type=pl.DeviceIdType.MESH
        )
    kcopies = [pltpu.make_async_copy(k_hbm.at[:, h], kbuf.at[h], ksem.at[h]) for h in range(kv)]
    vcopies = [pltpu.make_async_copy(v_hbm.at[:, h], vbuf.at[h], vsem.at[h]) for h in range(kv)]
    for h in range(kv):
        kcopies[h].start()
        vcopies[h].start()

    queries = q_ref[...].astype(F32).reshape(rows, kv, group, width)
    for h in range(kv):
        qall[h, 0:block, :] = queries[:, h].reshape(block, width).astype(BF16)

    span = owner_ref.shape[1]
    row = iota((rows, span), 0)
    length = jnp.zeros((rows, span), jnp.int32)
    for r in range(rows):
        length = jnp.where(row == r, lens_ref[r], length)
    live = jnp.clip(length - iota((rows, span), 1) * tokens, 0, tokens)
    live_f = live.astype(F32)
    owner = owner_ref[...]
    slot = slot_ref[...]
    ones = jnp.ones((8, span), BF16)
    slot_id = iota((pool, span), 0)
    for off in range(n):
        there = lax.rem(me + off, n)
        key = jnp.where((owner == there) & (live > 0), slot, -1)
        acc_live = jnp.zeros((pool, span), F32)
        acc_req = jnp.zeros((pool, span), F32)
        for r in range(rows):
            hit = slot_id == key[r : r + 1, :]
            acc_live = jnp.where(hit, live_f[r : r + 1, :], acc_live)
            acc_req = jnp.where(hit, float(r + 1), acc_req)
        t_live = lax.dot_general(ones, acc_live.astype(BF16), NT, preferred_element_type=F32)
        t_req = lax.dot_general(ones, acc_req.astype(BF16), NT, preferred_element_type=F32)
        table = jnp.where(iota((8, pool), 0) == 0, t_live, t_req)
        if lanes > pool:
            table = jnp.concatenate([table, jnp.zeros((8, lanes - pool), F32)], axis=1)
        if off == 0:
            trecv[0] = table
        else:
            tsend[off] = table

    pl.semaphore_wait(barrier, n - 1)
    tcopies = {}
    qcopies = {}
    for off in range(1, n):
        tcopies[off] = remote(
            tsend.at[off], trecv.at[off], tss.at[off], trs.at[off], peer(off)
        )
        tcopies[off].start()
    for h in range(kv):
        for off in range(1, n):
            qcopies[h, off] = remote(
                qall.at[h, pl.ds(0, block)],
                qall.at[h, pl.ds(off * block, block)],
                qss.at[h, off], qrs.at[h, off], peer(off),
            )
            qcopies[h, off].start()

    for off in range(1, n):
        tcopies[off].wait_recv()
    live_row = trecv[0][0:1, :]
    req_row = trecv[0][1:2, :]
    for off in range(1, n):
        t = trecv[off]
        live_row = live_row + t[0:1, :]
        req_row = req_row + jnp.where(t[1:2, :] > 0.0, t[1:2, :] + float(off * rows), 0.0)
    pg = pool * group
    spread = jnp.where(iota((pg, lanes), 0) // group == iota((pg, lanes), 1), 1.0, 0.0)
    spread = spread.astype(BF16)
    liveb[...] = lax.dot_general(
        spread, jnp.broadcast_to(live_row, (128, lanes)).astype(BF16), NT,
        preferred_element_type=F32,
    )
    reqb[...] = lax.dot_general(
        spread, jnp.broadcast_to(req_row, (128, lanes)).astype(BF16), NT,
        preferred_element_type=F32,
    )
    same = iota((pg, 128), 0) % group == iota((pg, 128), 1) % group
    for c in range(n * block // 128):
        want = ((iota((pg, 128), 1) + c * 128) // group + 1).astype(F32)
        mt[:, c * 128 : (c + 1) * 128] = jnp.where(
            same & (reqb[...] == want), 1.0, 0.0
        ).astype(BF16)
    spread_t = jnp.where(iota((lanes, pg), 0) == iota((lanes, pg), 1) // group, 1.0, 0.0)
    req_wide = jnp.dot(
        jnp.broadcast_to(req_row, (8, lanes)).astype(BF16), spread_t.astype(BF16),
        preferred_element_type=F32,
    )[0:1, :]
    same_t = iota((block, pg), 0) % group == iota((block, pg), 1) % group
    for off in range(n):
        want = (iota((block, pg), 0) // group + (off * rows + 1)).astype(F32)
        m[off * block : (off + 1) * block, :] = jnp.where(
            same_t & (req_wide == want), 1.0, 0.0
        ).astype(BF16)

    lane_f = iota((group, 128), 1).astype(F32)
    tops = []
    sums = []
    ocopies = {}
    for h in range(kv):
        for off in range(1, n):
            qcopies[h, off].wait_recv()
        qslot[...] = jnp.dot(mt[...], qall[h], preferred_element_type=F32)
        kcopies[h].wait()

        def pages(i, top):
            for u in range(unroll):
                p = i * unroll + u
                at = pl.ds(pl.multiple_of(p * group, group), group)
                s = lax.dot_general(
                    qslot[at, :].astype(BF16), kbuf[h, p], NT, preferred_element_type=F32
                )
                s = jnp.where(lane_f < liveb[at, :], s * scale, MASKED)
                pm = jnp.max(s, axis=1, keepdims=True)
                w = jnp.exp(s - pm)
                total = jnp.sum(w, axis=1, keepdims=True)
                wbuf[at, :] = w
                pmb[at, :] = jnp.broadcast_to(pm, (group, 128))
                lb[at, :] = jnp.broadcast_to(total, (group, 128))
                top = jnp.maximum(top, jnp.where(reqb[at, :] == lane_f + 1.0, pm, MASKED))
            return top

        top = lax.fori_loop(0, pool // unroll, pages, jnp.full((group, 128), MASKED, F32))
        vcopies[h].wait()

        def merge(i, acc):
            for u in range(unroll):
                p = i * unroll + u
                at = pl.ds(pl.multiple_of(p * group, group), group)
                out = jnp.dot(wbuf[at, :].astype(BF16), vbuf[h, p], preferred_element_type=F32)
                mine = reqb[at, :] == lane_f + 1.0
                rm = jnp.max(jnp.where(mine, top, MASKED), axis=1, keepdims=True)
                sc = jnp.exp(jnp.minimum(pmb[at, :] - rm, 0.0))
                ohi[at, :] = out * sc
                acc = acc + jnp.where(mine, sc * lb[at, :], 0.0)
            return acc

        acc = lax.fori_loop(0, pool // unroll, merge, jnp.zeros((group, 128), F32))
        osend[h] = jnp.dot(
            m[...], ohi[...].astype(BF16), preferred_element_type=F32
        ).astype(BF16)
        for off in range(1, n):
            ocopies[h, off] = remote(
                osend.at[h, pl.ds(off * block, block)], orecv.at[h, off],
                oss.at[h, off], ors.at[h, off], source(off),
            )
            ocopies[h, off].start()
        tops.append(top)
        sums.append(acc)

    lane = iota((group, 128), 1)
    scopies = {}
    for off in range(n):
        stat = jnp.zeros((group, 128), F32)
        for h in range(kv):
            for j, x in enumerate((tops[h], sums[h])):
                at = (2 * h + j) * rows
                shift = (at - off * rows) % 128
                y = pltpu.roll(x, shift, 1) if shift else x
                stat = jnp.where((lane >= at) & (lane < at + rows), y, stat)
        if off == 0:
            srecv[0] = stat
        else:
            ssend[off] = stat
            scopies[off] = remote(
                ssend.at[off], srecv.at[off], sss.at[off], srs.at[off], source(off)
            )
            scopies[off].start()

    for off in range(1, n):
        scopies[off].wait_recv()
    stats = [srecv[off] for off in range(n)]
    best = functools.reduce(jnp.maximum, stats)
    factors = [jnp.exp(x - best) for x in stats]
    whole = functools.reduce(
        jnp.add, [f * pltpu.roll(x, 128 - rows, 1) for f, x in zip(factors, stats)]
    )
    factors = [f / whole for f in factors]
    parts = []
    for h in range(kv):
        gathered = []
        for off in range(n):
            if off == 0:
                got = osend[h, 0:block, :]
            else:
                ocopies[h, off].wait_recv()
                got = orecv[h, off]
            gathered.append(got.astype(F32).reshape(rows, group, width))
        per_row = []
        for r in range(rows):
            at = 2 * h * rows + r
            total = factors[0][:, at : at + 1] * gathered[0][r]
            for off in range(1, n):
                total = total + factors[off][:, at : at + 1] * gathered[off][r]
            per_row.append(total)
        parts.append(per_row)
    for r in range(rows):
        out_ref[r] = jnp.concatenate([parts[h][r] for h in range(kv)], axis=0).astype(BF16)

    for off in range(1, n):
        tcopies[off].wait_send()
        scopies[off].wait_send()
        for h in range(kv):
            qcopies[h, off].wait_send()
            ocopies[h, off].wait_send()


def on_device(n, queries, page_owner, page_slot, lengths, keys, values):
    pool, kv, tokens, width = keys.shape
    rows, heads, _ = queries.shape
    group = heads // kv
    block = rows * group
    pg = pool * group
    lanes = -(-pool // 128) * 128
    unroll = math.gcd(pool, 16)
    dma = pltpu.SemaphoreType.DMA
    vmem = pl.BlockSpec(memory_space=pltpu.VMEM)
    return pl.pallas_call(
        functools.partial(kernel, n, unroll),
        out_shape=jax.ShapeDtypeStruct(queries.shape, BF16),
        in_specs=[
            pl.BlockSpec(memory_space=pltpu.SMEM),
            vmem,
            vmem,
            vmem,
            pl.BlockSpec(memory_space=pl.ANY),
            pl.BlockSpec(memory_space=pl.ANY),
        ],
        out_specs=vmem,
        scratch_shapes=[
            pltpu.VMEM((kv, pool, tokens, width), BF16),
            pltpu.VMEM((kv, pool, tokens, width), BF16),
            pltpu.VMEM((kv, n * block, width), BF16),
            pltpu.VMEM((n, 8, lanes), F32),
            pltpu.VMEM((n, 8, lanes), F32),
            pltpu.VMEM((pg, 128), F32),
            pltpu.VMEM((pg, 128), F32),
            pltpu.VMEM((pg, n * block), BF16),
            pltpu.VMEM((n * block, pg), BF16),
            pltpu.VMEM((pg, width), F32),
            pltpu.VMEM((pg, 128), F32),
            pltpu.VMEM((pg, 128), F32),
            pltpu.VMEM((pg, width), F32),
            pltpu.VMEM((pg, width), F32),
            pltpu.VMEM((kv, n * block, width), BF16),
            pltpu.VMEM((kv, n, block, width), BF16),
            pltpu.VMEM((n, group, 128), F32),
            pltpu.VMEM((n, group, 128), F32),
            dma((kv,)), dma((kv,)),
            dma((n,)), dma((n,)),
            dma((kv, n)), dma((kv, n)),
            dma((kv, n)), dma((kv, n)),
            dma((n,)), dma((n,)),
        ],
        compiler_params=pltpu.CompilerParams(
            collective_id=0, has_side_effects=True, vmem_limit_bytes=60 * 1024 * 1024
        ),
        name="paged",
    )(lengths, queries, page_owner, page_slot, keys, values)


def solution(mesh):
    placed = (
        P(("groups", "seq", "rep"), "head", None),
        P(("groups", "seq", "rep"), None),
        P(("groups", "seq", "rep"), None),
        P(("groups", "seq", "rep")),
        P(("groups", "seq", "rep"), "head", None, None),
        P(("groups", "seq", "rep"), "head", None, None),
    )
    return jax.shard_map(
        functools.partial(on_device, mesh.shape["seq"]),
        mesh=mesh,
        in_specs=placed,
        out_specs=P(("groups", "seq", "rep"), "head", None),
        check_vma=False,
    )
```

profile of v0, /device:TPU:0, one launch (start us, length us, event | category | flops | bytes accessed | tf_op | source)
XLA Modules:
  0.0 33.1 jit_solution(12891530724375483285)
XLA Ops:
  0.0 31.7 %paged.1 = bf16[8,32,128]{2,1,0:T(8,128)(2,1)} custom-call(s32[8]{0:T(128)} %lens_ref.1, bf16[8,32,128]{2,1,0:T(8,128)(2,1)} %q_ref.1, s32[8,128]{1,0:T(8,128)} %owner_ref.1, s32[8,128]{1,0:T(8,128)} %slot_ref.1, bf16[64,4,128,128]{3,2,1,0:T(8,128)(2,1)} %k_hbm.1, bf16[64,4,128,128]{3,2,1,0:T(8,128)(2,1)} %v_hbm.1), custom_call_target="tpu_custom_call" | custom-call | tf_op jit(solution)/shard_map/paged/pallas_call | solution.py:268
  31.7 1.5 %copy.8 = bf16[8,32,128]{2,1,0:T(8,128)(2,1)} copy(bf16[8,32,128]{2,1,0:T(8,128)(2,1)} %paged.1) | data formatting | bytes 131072
where the time goes:
time: 33.3 us; the launch traced here: 33.1 us
  Pallas kernels  31.7 us (95%)
  local copies, waits for them, and re-layouts  1.47 us (4%)
    pallas_call x1, Pallas kernels, on_device(): pl.pallas_call(functools.partial(kernel, n, unroll), out_shape=jax.ShapeD...  31.7 us
    unnamed x1, local copies, waits for them, and re-layouts  1.47 us

commit v1 on v0

--- a/solution.py
+++ b/solution.py
@@ -19,8 +19,8 @@
 
 
 def kernel(
-    n, unroll, lens_ref, q_ref, owner_ref, slot_ref, k_hbm, v_hbm, out_ref,
-    kbuf, vbuf, qall, tsend, trecv, liveb, reqb, mt, m, qslot, pmb, lb, wbuf, ohi,
+    n, lens_ref, q_ref, owner_ref, slot_ref, k_hbm, v_hbm, out_ref,
+    kbuf, vbuf, qall, tsend, trecv, liveb, reqb, mt, m, qslot, wbuf, ohi,
     osend, orecv, ssend, srecv,
     ksem, vsem, tss, trs, qss, qrs, oss, ors, sss, srs,
 ):
@@ -29,7 +29,7 @@
     group = q_ref.shape[1] // kv
     block = rows * group
     lanes = trecv.shape[2]
-    scale = 1.0 / math.sqrt(width)
+    scale = math.log2(math.e) / math.sqrt(width)
     me = lax.axis_index("seq")
 
     def peer(off):
@@ -144,84 +144,83 @@
         ).astype(BF16)
 
     lane_f = iota((group, 128), 1).astype(F32)
+    lane = iota((group, 128), 1)
+    pair = 2 * group
     tops = []
     sums = []
     ocopies = {}
+    scopies = {}
     for h in range(kv):
         for off in range(1, n):
             qcopies[h, off].wait_recv()
-        qslot[...] = jnp.dot(mt[...], qall[h], preferred_element_type=F32)
+        qslot[...] = jnp.dot(mt[...], qall[h], preferred_element_type=F32).astype(BF16)
         kcopies[h].wait()
 
-        def pages(i, top):
-            for u in range(unroll):
-                p = i * unroll + u
-                at = pl.ds(pl.multiple_of(p * group, group), group)
-                s = lax.dot_general(
-                    qslot[at, :].astype(BF16), kbuf[h, p], NT, preferred_element_type=F32
-                )
-                s = jnp.where(lane_f < liveb[at, :], s * scale, MASKED)
-                pm = jnp.max(s, axis=1, keepdims=True)
-                w = jnp.exp(s - pm)
-                total = jnp.sum(w, axis=1, keepdims=True)
-                wbuf[at, :] = w
-                pmb[at, :] = jnp.broadcast_to(pm, (group, 128))
-                lb[at, :] = jnp.broadcast_to(total, (group, 128))
+        top = jnp.full((group, 128), MASKED, F32)
+        for i in range(pool // 2):
+            keys = kbuf[h, 2 * i : 2 * i + 2].reshape(2 * tokens, width)
+            s = lax.dot_general(
+                qslot[i * pair : (i + 1) * pair, :], keys, NT, preferred_element_type=F32
+            )
+            for u in range(2):
+                at = slice((2 * i + u) * group, (2 * i + u + 1) * group)
+                x = s[u * group : (u + 1) * group, u * tokens : (u + 1) * tokens]
+                x = jnp.where(lane_f < liveb[at, :], x * scale, MASKED)
+                wbuf[at, :] = x
+                pm = jnp.max(x, axis=1, keepdims=True)
                 top = jnp.maximum(top, jnp.where(reqb[at, :] == lane_f + 1.0, pm, MASKED))
-            return top
-
-        top = lax.fori_loop(0, pool // unroll, pages, jnp.full((group, 128), MASKED, F32))
         vcopies[h].wait()
 
-        def merge(i, acc):
-            for u in range(unroll):
-                p = i * unroll + u
-                at = pl.ds(pl.multiple_of(p * group, group), group)
-                out = jnp.dot(wbuf[at, :].astype(BF16), vbuf[h, p], preferred_element_type=F32)
+        acc = jnp.zeros((group, 128), F32)
+        for i in range(pool // 2):
+            weights = []
+            for u in range(2):
+                at = slice((2 * i + u) * group, (2 * i + u + 1) * group)
                 mine = reqb[at, :] == lane_f + 1.0
                 rm = jnp.max(jnp.where(mine, top, MASKED), axis=1, keepdims=True)
-                sc = jnp.exp(jnp.minimum(pmb[at, :] - rm, 0.0))
-                ohi[at, :] = out * sc
-                acc = acc + jnp.where(mine, sc * lb[at, :], 0.0)
-            return acc
-
-        acc = lax.fori_loop(0, pool // unroll, merge, jnp.zeros((group, 128), F32))
-        osend[h] = jnp.dot(
-            m[...], ohi[...].astype(BF16), preferred_element_type=F32
-        ).astype(BF16)
+                w = jnp.exp2(wbuf[at, :] - rm)
+                acc = acc + jnp.where(mine, jnp.sum(w, axis=1, keepdims=True), 0.0)
+                weights.append(w)
+            both = jnp.concatenate([vbuf[h, 2 * i], vbuf[h, 2 * i + 1]], axis=1)
+            out = jnp.dot(
+                jnp.concatenate(weights, axis=0).astype(BF16), both, preferred_element_type=F32
+            )
+            ohi[i * pair : (i + 1) * pair, :] = jnp.concatenate(
+                [out[u * group : (u + 1) * group, u * width : (u + 1) * width] for u in range(2)],
+                axis=0,
+            ).astype(BF16)
+        tops.append(top)
+        sums.append(acc)
+        if h == kv - 1:
+            for off in range(n):
+                stat = jnp.zeros((group, 128), F32)
+                for g in range(kv):
+                    for j, x in enumerate((tops[g], sums[g])):
+                        at = (2 * g + j) * rows
+                        shift = (at - off * rows) % 128
+                        y = pltpu.roll(x, shift, 1) if shift else x
+                        stat = jnp.where((lane >= at) & (lane < at + rows), y, stat)
+                if off == 0:
+                    srecv[0] = stat
+                else:
+                    ssend[off] = stat
+                    scopies[off] = remote(
+                        ssend.at[off], srecv.at[off], sss.at[off], srs.at[off], source(off)
+                    )
+                    scopies[off].start()
+        osend[h] = jnp.dot(m[...], ohi[...], preferred_element_type=F32).astype(BF16)
         for off in range(1, n):
             ocopies[h, off] = remote(
                 osend.at[h, pl.ds(off * block, block)], orecv.at[h, off],
                 oss.at[h, off], ors.at[h, off], source(off),
             )
             ocopies[h, off].start()
-        tops.append(top)
-        sums.append(acc)
-
-    lane = iota((group, 128), 1)
-    scopies = {}
-    for off in range(n):
-        stat = jnp.zeros((group, 128), F32)
-        for h in range(kv):
-            for j, x in enumerate((tops[h], sums[h])):
-                at = (2 * h + j) * rows
-                shift = (at - off * rows) % 128
-                y = pltpu.roll(x, shift, 1) if shift else x
-                stat = jnp.where((lane >= at) & (lane < at + rows), y, stat)
-        if off == 0:
-            srecv[0] = stat
-        else:
-            ssend[off] = stat
-            scopies[off] = remote(
-                ssend.at[off], srecv.at[off], sss.at[off], srs.at[off], source(off)
-            )
-            scopies[off].start()
 
     for off in range(1, n):
         scopies[off].wait_recv()
     stats = [srecv[off] for off in range(n)]
     best = functools.reduce(jnp.maximum, stats)
-    factors = [jnp.exp(x - best) for x in stats]
+    factors = [jnp.exp2(x - best) for x in stats]
     whole = functools.reduce(
         jnp.add, [f * pltpu.roll(x, 128 - rows, 1) for f, x in zip(factors, stats)]
     )
@@ -262,11 +261,10 @@
     block = rows * group
     pg = pool * group
     lanes = -(-pool // 128) * 128
-    unroll = math.gcd(pool, 16)
     dma = pltpu.SemaphoreType.DMA
     vmem = pl.BlockSpec(memory_space=pltpu.VMEM)
     return pl.pallas_call(
-        functools.partial(kernel, n, unroll),
+        functools.partial(kernel, n),
         out_shape=jax.ShapeDtypeStruct(queries.shape, BF16),
         in_specs=[
             pl.BlockSpec(memory_space=pltpu.SMEM),
@@ -287,11 +285,9 @@
             pltpu.VMEM((pg, 128), F32),
             pltpu.VMEM((pg, n * block), BF16),
             pltpu.VMEM((n * block, pg), BF16),
-            pltpu.VMEM((pg, width), F32),
-            pltpu.VMEM((pg, 128), F32),
-            pltpu.VMEM((pg, 128), F32),
-            pltpu.VMEM((pg, width), F32),
-            pltpu.VMEM((pg, width), F32),
+            pltpu.VMEM((pg, width), BF16),
+            pltpu.VMEM((pg, tokens), F32),
+            pltpu.VMEM((pg, width), BF16),
             pltpu.VMEM((kv, n * block, width), BF16),
             pltpu.VMEM((kv, n, block, width), BF16),
             pltpu.VMEM((n, group, 128), F32),

time: 33.3 us -> 25.1 us (0.75)
  Pallas kernels: 31.7 us -> 23.5 us
    pallas_call x1, Pallas kernels: 31.7 us -> 23.5 us  [on_device(): pl.pallas_call(functools.partial(kernel, n), out_shape=jax.ShapeDtypeStru...]
where the time goes in v1:
time: 25.1 us; the launch traced here: 24.9 us
  Pallas kernels  23.5 us (94%)
  local copies, waits for them, and re-layouts  1.47 us (6%)
    pallas_call x1, Pallas kernels, on_device(): pl.pallas_call(functools.partial(kernel, n), out_shape=jax.ShapeDtypeStru...  23.5 us
    unnamed x1, local copies, waits for them, and re-layouts  1.47 us

profile of v1, /device:TPU:0, one launch (start us, length us, event | category | flops | bytes accessed | tf_op | source)
XLA Modules:
  0.0 24.9 jit_solution(6456800419465465985)
XLA Ops:
  0.0 23.5 %paged.1 = bf16[8,32,128]{2,1,0:T(8,128)(2,1)} custom-call(s32[8]{0:T(128)} %lens_ref.1, bf16[8,32,128]{2,1,0:T(8,128)(2,1)} %q_ref.1, s32[8,128]{1,0:T(8,128)} %owner_ref.1, s32[8,128]{1,0:T(8,128)} %slot_ref.1, bf16[64,4,128,128]{3,2,1,0:T(8,128)(2,1)} %k_hbm.1, bf16[64,4,128,128]{3,2,1,0:T(8,128)(2,1)} %v_hbm.1), custom_call_target="tpu_custom_call" | custom-call | tf_op jit(solution)/shard_map/paged/pallas_call | solution.py:266
  23.5 1.5 %copy.8 = bf16[8,32,128]{2,1,0:T(8,128)(2,1)} copy(bf16[8,32,128]{2,1,0:T(8,128)(2,1)} %paged.1) | data formatting | bytes 131072

commit v2 on v1

--- a/solution.py
+++ b/solution.py
@@ -19,14 +19,14 @@
 
 
 def kernel(
-    n, lens_ref, q_ref, owner_ref, slot_ref, k_hbm, v_hbm, out_ref,
-    kbuf, vbuf, qall, tsend, trecv, liveb, reqb, mt, m, qslot, wbuf, ohi,
+    n, lens_hbm, q_hbm, owner_hbm, slot_hbm, k_hbm, v_hbm, out_ref,
+    lens_ref, q_ref, owner_ref, slot_ref, kbuf, vbuf, qall, tsend, trecv, liveb, reqb, mt, m, qslot, wbuf, ohi,
     osend, orecv, ssend, srecv,
-    ksem, vsem, tss, trs, qss, qrs, oss, ors, sss, srs,
+    isem, ksem, vsem, tss, trs, qss, qrs, oss, ors, sss, srs,
 ):
     pool, kv, tokens, width = k_hbm.shape
-    rows = q_ref.shape[0]
-    group = q_ref.shape[1] // kv
+    rows = q_hbm.shape[0]
+    group = q_hbm.shape[1] // kv
     block = rows * group
     lanes = trecv.shape[2]
     scale = math.log2(math.e) / math.sqrt(width)
@@ -49,16 +49,22 @@
         pl.semaphore_signal(
             barrier, inc=1, device_id=peer(off), device_id_type=pl.DeviceIdType.MESH
         )
+    icopies = [
+        pltpu.make_async_copy(src, dst, isem.at[i])
+        for i, (src, dst) in enumerate((
+            (lens_hbm, lens_ref), (owner_hbm, owner_ref), (slot_hbm, slot_ref), (q_hbm, q_ref),
+        ))
+    ]
+    for copy in icopies:
+        copy.start()
     kcopies = [pltpu.make_async_copy(k_hbm.at[:, h], kbuf.at[h], ksem.at[h]) for h in range(kv)]
     vcopies = [pltpu.make_async_copy(v_hbm.at[:, h], vbuf.at[h], vsem.at[h]) for h in range(kv)]
+
+    for copy in icopies:
+        copy.wait()
     for h in range(kv):
         kcopies[h].start()
         vcopies[h].start()
-
-    queries = q_ref[...].astype(F32).reshape(rows, kv, group, width)
-    for h in range(kv):
-        qall[h, 0:block, :] = queries[:, h].reshape(block, width).astype(BF16)
-
     span = owner_ref.shape[1]
     row = iota((rows, span), 0)
     length = jnp.zeros((rows, span), jnp.int32)
@@ -89,6 +95,10 @@
         else:
             tsend[off] = table
 
+    queries = q_ref[...].astype(F32).reshape(rows, kv, group, width)
+    for h in range(kv):
+        qall[h, 0:block, :] = queries[:, h].reshape(block, width).astype(BF16)
+
     pl.semaphore_wait(barrier, n - 1)
     tcopies = {}
     qcopies = {}
@@ -104,10 +114,25 @@
                 qall.at[h, pl.ds(off * block, block)],
                 qss.at[h, off], qrs.at[h, off], peer(off),
             )
-            qcopies[h, off].start()
+
+    def send(first, last):
+        for h in range(first, last):
+            for off in range(1, n):
+                qcopies[h, off].start()
+
+    early = lax.axis_index("rep") == 0
+
+    @pl.when(early)
+    def _():
+        send(0, kv)
 
     for off in range(1, n):
         tcopies[off].wait_recv()
+
+    @pl.when(jnp.logical_not(early))
+    def _():
+        send(0, kv)
+
     live_row = trecv[0][0:1, :]
     req_row = trecv[0][1:2, :]
     for off in range(1, n):
@@ -265,17 +290,14 @@
     vmem = pl.BlockSpec(memory_space=pltpu.VMEM)
     return pl.pallas_call(
         functools.partial(kernel, n),
-        out_shape=jax.ShapeDtypeStruct(queries.shape, BF16),
-        in_specs=[
-            pl.BlockSpec(memory_space=pltpu.SMEM),
-            vmem,
-            vmem,
-            vmem,
-            pl.BlockSpec(memory_space=pl.ANY),
-            pl.BlockSpec(memory_space=pl.ANY),
-        ],
+        out_shape=pltpu.VMEM(queries.shape, BF16),
+        in_specs=[pl.BlockSpec(memory_space=pl.ANY)] * 6,
         out_specs=vmem,
         scratch_shapes=[
+            pltpu.SMEM(lengths.shape, jnp.int32),
+            pltpu.VMEM(queries.shape, BF16),
+            pltpu.VMEM(page_owner.shape, jnp.int32),
+            pltpu.VMEM(page_slot.shape, jnp.int32),
             pltpu.VMEM((kv, pool, tokens, width), BF16),
             pltpu.VMEM((kv, pool, tokens, width), BF16),
             pltpu.VMEM((kv, n * block, width), BF16),
@@ -292,14 +314,14 @@
             pltpu.VMEM((kv, n, block, width), BF16),
             pltpu.VMEM((n, group, 128), F32),
             pltpu.VMEM((n, group, 128), F32),
-            dma((kv,)), dma((kv,)),
+            dma((4,)), dma((kv,)), dma((kv,)),
             dma((n,)), dma((n,)),
             dma((kv, n)), dma((kv, n)),
             dma((kv, n)), dma((kv, n)),
             dma((n,)), dma((n,)),
         ],
         compiler_params=pltpu.CompilerParams(
-            collective_id=0, has_side_effects=True, vmem_limit_bytes=60 * 1024 * 1024
+            collective_id=0, has_side_effects=True, vmem_limit_bytes=66977792
         ),
         name="paged",
     )(lengths, queries, page_owner, page_slot, keys, values)

time: 25.1 us -> 22.3 us (0.89)
  the two profiles are of different devices: /device:TPU:0 before, /device:TPU:1 now
where the time goes in v2:
time: 22.3 us; the launch traced here: 22.1 us
  Pallas kernels  21.5 us (96%)
  local copies, waits for them, and re-layouts  0.63 us (3%)
    pallas_call x1, Pallas kernels, on_device(): pl.pallas_call(functools.partial(kernel, n), out_shape=pltpu.VMEM(queries...  21.5 us
    unnamed x1, local copies, waits for them, and re-layouts  0.63 us

profile of v2, /device:TPU:1, one launch (start us, length us, event | category | flops | bytes accessed | tf_op | source)
XLA Modules:
  0.0 22.1 jit_solution(2153287920061528187)
XLA Ops:
  0.0 21.5 %paged.1 = bf16[8,32,128]{2,1,0:T(8,128)(2,1)S(1)} custom-call(s32[8]{0:T(128)} %lens_hbm.1, bf16[8,32,128]{2,1,0:T(8,128)(2,1)} %q_hbm.1, s32[8,128]{1,0:T(8,128)} %owner_hbm.1, s32[8,128]{1,0:T(8,128)} %slot_hbm.1, bf16[64,4,128,128]{3,2,1,0:T(8,128)(2,1)} %k_hbm.1, bf16[64,4,128,128]{3,2,1,0:T(8,128)(2,1)} %v_hbm.1), custom_call_target="tpu_custom_call" | custom-call | tf_op jit(solution)/shard_map/paged/pallas_call | solution.py:291
  21.5 0.6 %copy.8 = bf16[8,32,128]{2,1,0:T(8,128)(2,1)} copy(bf16[8,32,128]{2,1,0:T(8,128)(2,1)S(1)} %paged.1) | data formatting | bytes 131072

commit v3 on v2

--- a/solution.py
+++ b/solution.py
@@ -9,6 +9,9 @@
 from jax.sharding import PartitionSpec as P
 
 MASKED = -1e30
+CODE = 256.0
+LATE = 0
+DEPTH = 3
 F32 = jnp.float32
 BF16 = jnp.bfloat16
 NT = (((1,), (1,)), ((), ()))
@@ -44,6 +47,12 @@
             device_id=to, device_id_type=pl.DeviceIdType.MESH,
         )
 
+    def landed(ref, sem):
+        remote(ref, ref, sem, sem, peer(1)).wait_recv()
+
+    def sent(ref, sem):
+        remote(ref, ref, sem, sem, peer(1)).wait_send()
+
     barrier = pltpu.get_barrier_semaphore()
     for off in range(1, n):
         pl.semaphore_signal(
@@ -62,9 +71,9 @@
 
     for copy in icopies:
         copy.wait()
-    for h in range(kv):
-        kcopies[h].start()
-        vcopies[h].start()
+    loads = kcopies + vcopies
+    for copy in loads[:DEPTH]:
+        copy.start()
     span = owner_ref.shape[1]
     row = iota((rows, span), 0)
     length = jnp.zeros((rows, span), jnp.int32)
@@ -87,9 +96,9 @@
             acc_req = jnp.where(hit, float(r + 1), acc_req)
         t_live = lax.dot_general(ones, acc_live.astype(BF16), NT, preferred_element_type=F32)
         t_req = lax.dot_general(ones, acc_req.astype(BF16), NT, preferred_element_type=F32)
-        table = jnp.where(iota((8, pool), 0) == 0, t_live, t_req)
+        table = (t_req * CODE + t_live)[0:1, :]
         if lanes > pool:
-            table = jnp.concatenate([table, jnp.zeros((8, lanes - pool), F32)], axis=1)
+            table = jnp.concatenate([table, jnp.zeros((1, lanes - pool), F32)], axis=1)
         if off == 0:
             trecv[0] = table
         else:
@@ -104,7 +113,7 @@
     qcopies = {}
     for off in range(1, n):
         tcopies[off] = remote(
-            tsend.at[off], trecv.at[off], tss.at[off], trs.at[off], peer(off)
+            tsend.at[off], trecv.at[off], tss, trs, peer(off)
         )
         tcopies[off].start()
     for h in range(kv):
@@ -112,7 +121,7 @@
             qcopies[h, off] = remote(
                 qall.at[h, pl.ds(0, block)],
                 qall.at[h, pl.ds(off * block, block)],
-                qss.at[h, off], qrs.at[h, off], peer(off),
+                qss, qrs.at[h], peer(off),
             )
 
     def send(first, last):
@@ -126,19 +135,32 @@
     def _():
         send(0, kv)
 
-    for off in range(1, n):
-        tcopies[off].wait_recv()
-
-    @pl.when(jnp.logical_not(early))
-    def _():
-        send(0, kv)
-
-    live_row = trecv[0][0:1, :]
-    req_row = trecv[0][1:2, :]
-    for off in range(1, n):
+    step = math.gcd(pool, 16)
+    for h in range(kv):
+        kcopies[h].wait()
+        for copy in loads[DEPTH + h :] if h == kv - 1 else loads[DEPTH + h : DEPTH + h + 1]:
+            copy.start()
+
+        def turn(i, carry):
+            for u in range(step):
+                kbuf[h, i * step + u] = kbuf[h, i * step + u].T
+            return carry
+
+        lax.fori_loop(0, pool // step, turn, 0)
+        if h == LATE:
+
+            @pl.when(jnp.logical_not(early))
+            def _():
+                send(0, kv)
+
+    landed(trecv.at[pl.ds(1, n - 1)], trs)
+    live_row = jnp.zeros((1, lanes), F32)
+    req_row = jnp.zeros((1, lanes), F32)
+    for off in range(n):
         t = trecv[off]
-        live_row = live_row + t[0:1, :]
-        req_row = req_row + jnp.where(t[1:2, :] > 0.0, t[1:2, :] + float(off * rows), 0.0)
+        request = jnp.floor(t * (1.0 / CODE))
+        live_row = live_row + (t - request * CODE)
+        req_row = req_row + jnp.where(request > 0.0, request + float(off * rows), 0.0)
     pg = pool * group
     spread = jnp.where(iota((pg, lanes), 0) // group == iota((pg, lanes), 1), 1.0, 0.0)
     spread = spread.astype(BF16)
@@ -171,78 +193,101 @@
     lane_f = iota((group, 128), 1).astype(F32)
     lane = iota((group, 128), 1)
     pair = 2 * group
-    tops = []
-    sums = []
+    pairs = pool // 2
+    ahead = min(8, pairs)
+    tops = [jnp.full((group, 128), MASKED, F32) for _ in range(kv)]
+    sums = [jnp.zeros((group, 128), F32) for _ in range(kv)]
     ocopies = {}
     scopies = {}
-    for h in range(kv):
-        for off in range(1, n):
-            qcopies[h, off].wait_recv()
-        qslot[...] = jnp.dot(mt[...], qall[h], preferred_element_type=F32).astype(BF16)
-        kcopies[h].wait()
-
-        top = jnp.full((group, 128), MASKED, F32)
-        for i in range(pool // 2):
-            keys = kbuf[h, 2 * i : 2 * i + 2].reshape(2 * tokens, width)
-            s = lax.dot_general(
-                qslot[i * pair : (i + 1) * pair, :], keys, NT, preferred_element_type=F32
+
+    def gather(h):
+        landed(qall.at[h, pl.ds(block, (n - 1) * block)], qrs.at[h])
+        half = pool * group // 2
+        for u in range(2):
+            at = slice(u * half, (u + 1) * half)
+            qslot[h % 2, at, :] = jnp.dot(
+                mt[at, :], qall[h], preferred_element_type=F32
+            ).astype(BF16)
+
+    def score(h, i):
+        keys = jnp.concatenate([kbuf[h, 2 * i], kbuf[h, 2 * i + 1]], axis=1)
+        s = jnp.dot(
+            qslot[h % 2, i * pair : (i + 1) * pair, :], keys, preferred_element_type=F32
+        )
+        for u in range(2):
+            at = slice((2 * i + u) * group, (2 * i + u + 1) * group)
+            x = s[u * group : (u + 1) * group, u * tokens : (u + 1) * tokens]
+            x = jnp.where(lane_f < liveb[at, :], x * scale, MASKED)
+            wbuf[h % 2, at, :] = x
+            pm = jnp.max(x, axis=1, keepdims=True)
+            tops[h] = jnp.maximum(
+                tops[h], jnp.where(reqb[at, :] == lane_f + 1.0, pm, MASKED)
             )
-            for u in range(2):
-                at = slice((2 * i + u) * group, (2 * i + u + 1) * group)
-                x = s[u * group : (u + 1) * group, u * tokens : (u + 1) * tokens]
-                x = jnp.where(lane_f < liveb[at, :], x * scale, MASKED)
-                wbuf[at, :] = x
-                pm = jnp.max(x, axis=1, keepdims=True)
-                top = jnp.maximum(top, jnp.where(reqb[at, :] == lane_f + 1.0, pm, MASKED))
-        vcopies[h].wait()
-
-        acc = jnp.zeros((group, 128), F32)
-        for i in range(pool // 2):
-            weights = []
-            for u in range(2):
-                at = slice((2 * i + u) * group, (2 * i + u + 1) * group)
-                mine = reqb[at, :] == lane_f + 1.0
-                rm = jnp.max(jnp.where(mine, top, MASKED), axis=1, keepdims=True)
-                w = jnp.exp2(wbuf[at, :] - rm)
-                acc = acc + jnp.where(mine, jnp.sum(w, axis=1, keepdims=True), 0.0)
-                weights.append(w)
-            both = jnp.concatenate([vbuf[h, 2 * i], vbuf[h, 2 * i + 1]], axis=1)
-            out = jnp.dot(
-                jnp.concatenate(weights, axis=0).astype(BF16), both, preferred_element_type=F32
-            )
-            ohi[i * pair : (i + 1) * pair, :] = jnp.concatenate(
-                [out[u * group : (u + 1) * group, u * width : (u + 1) * width] for u in range(2)],
-                axis=0,
-            ).astype(BF16)
-        tops.append(top)
-        sums.append(acc)
+
+    def weigh(h, i):
+        weights = []
+        for u in range(2):
+            at = slice((2 * i + u) * group, (2 * i + u + 1) * group)
+            mine = reqb[at, :] == lane_f + 1.0
+            rm = jnp.max(jnp.where(mine, tops[h], MASKED), axis=1, keepdims=True)
+            w = jnp.exp2(wbuf[h % 2, at, :] - rm)
+            sums[h] = sums[h] + jnp.where(mine, jnp.sum(w, axis=1, keepdims=True), 0.0)
+            weights.append(w)
+        both = jnp.concatenate([vbuf[h, 2 * i], vbuf[h, 2 * i + 1]], axis=1)
+        out = jnp.dot(
+            jnp.concatenate(weights, axis=0).astype(BF16), both, preferred_element_type=F32
+        )
+        ohi[i * pair : (i + 1) * pair, :] = jnp.concatenate(
+            [out[u * group : (u + 1) * group, u * width : (u + 1) * width] for u in range(2)],
+            axis=0,
+        ).astype(BF16)
+
+    def statistics():
+        for off in range(n):
+            stat = jnp.zeros((group, 128), F32)
+            for g in range(kv):
+                for j, x in enumerate((tops[g], sums[g])):
+                    at = (2 * g + j) * rows
+                    shift = (at - off * rows) % 128
+                    y = pltpu.roll(x, shift, 1) if shift else x
+                    stat = jnp.where((lane >= at) & (lane < at + rows), y, stat)
+            if off == 0:
+                srecv[0] = stat
+            else:
+                ssend[off] = stat
+                scopies[off] = remote(
+                    ssend.at[off], srecv.at[off], sss, srs, source(off)
+                )
+                scopies[off].start()
+
+    def finish(h):
         if h == kv - 1:
-            for off in range(n):
-                stat = jnp.zeros((group, 128), F32)
-                for g in range(kv):
-                    for j, x in enumerate((tops[g], sums[g])):
-                        at = (2 * g + j) * rows
-                        shift = (at - off * rows) % 128
-                        y = pltpu.roll(x, shift, 1) if shift else x
-                        stat = jnp.where((lane >= at) & (lane < at + rows), y, stat)
-                if off == 0:
-                    srecv[0] = stat
-                else:
-                    ssend[off] = stat
-                    scopies[off] = remote(
-                        ssend.at[off], srecv.at[off], sss.at[off], srs.at[off], source(off)
-                    )
-                    scopies[off].start()
+            statistics()
         osend[h] = jnp.dot(m[...], ohi[...], preferred_element_type=F32).astype(BF16)
         for off in range(1, n):
             ocopies[h, off] = remote(
                 osend.at[h, pl.ds(off * block, block)], orecv.at[h, off],
-                oss.at[h, off], ors.at[h, off], source(off),
+                oss, ors.at[h], source(off),
             )
             ocopies[h, off].start()
 
-    for off in range(1, n):
-        scopies[off].wait_recv()
+    gather(0)
+    for i in range(pairs):
+        score(0, i)
+    for h in range(kv):
+        vcopies[h].wait()
+        more = h + 1 < kv
+        if more:
+            gather(h + 1)
+        for i in range(pairs + ahead):
+            if more and i >= ahead:
+                score(h + 1, i - ahead)
+            if i < pairs:
+                weigh(h, i)
+            if i == pairs - 1:
+                finish(h)
+
+    landed(srecv.at[pl.ds(1, n - 1)], srs)
     stats = [srecv[off] for off in range(n)]
     best = functools.reduce(jnp.maximum, stats)
     factors = [jnp.exp2(x - best) for x in stats]
@@ -252,13 +297,10 @@
     factors = [f / whole for f in factors]
     parts = []
     for h in range(kv):
+        landed(orecv.at[h, pl.ds(1, n - 1)], ors.at[h])
         gathered = []
         for off in range(n):
-            if off == 0:
-                got = osend[h, 0:block, :]
-            else:
-                ocopies[h, off].wait_recv()
-                got = orecv[h, off]
+            got = orecv[h, off] if off else osend[h, 0:block, :]
             gathered.append(got.astype(F32).reshape(rows, group, width))
         per_row = []
         for r in range(rows):
@@ -271,12 +313,10 @@
     for r in range(rows):
         out_ref[r] = jnp.concatenate([parts[h][r] for h in range(kv)], axis=0).astype(BF16)
 
-    for off in range(1, n):
-        tcopies[off].wait_send()
-        scopies[off].wait_send()
-        for h in range(kv):
-            qcopies[h, off].wait_send()
-            ocopies[h, off].wait_send()
+    sent(trecv.at[pl.ds(1, n - 1)], tss)
+    sent(qall.at[:, pl.ds(block, (n - 1) * block)], qss)
+    sent(osend.at[:, pl.ds(block, (n - 1) * block)], oss)
+    sent(srecv.at[pl.ds(1, n - 1)], sss)
 
 
 def on_device(n, queries, page_owner, page_slot, lengths, keys, values):
@@ -301,24 +341,24 @@
             pltpu.VMEM((kv, pool, tokens, width), BF16),
             pltpu.VMEM((kv, pool, tokens, width), BF16),
             pltpu.VMEM((kv, n * block, width), BF16),
-            pltpu.VMEM((n, 8, lanes), F32),
-            pltpu.VMEM((n, 8, lanes), F32),
+            pltpu.VMEM((n, 1, lanes), F32),
+            pltpu.VMEM((n, 1, lanes), F32),
             pltpu.VMEM((pg, 128), F32),
             pltpu.VMEM((pg, 128), F32),
             pltpu.VMEM((pg, n * block), BF16),
             pltpu.VMEM((n * block, pg), BF16),
-            pltpu.VMEM((pg, width), BF16),
-            pltpu.VMEM((pg, tokens), F32),
+            pltpu.VMEM((2, pg, width), BF16),
+            pltpu.VMEM((2, pg, tokens), F32),
             pltpu.VMEM((pg, width), BF16),
             pltpu.VMEM((kv, n * block, width), BF16),
             pltpu.VMEM((kv, n, block, width), BF16),
             pltpu.VMEM((n, group, 128), F32),
             pltpu.VMEM((n, group, 128), F32),
             dma((4,)), dma((kv,)), dma((kv,)),
-            dma((n,)), dma((n,)),
-            dma((kv, n)), dma((kv, n)),
-            dma((kv, n)), dma((kv, n)),
-            dma((n,)), dma((n,)),
+            dma, dma,
+            dma, dma((kv,)),
+            dma, dma((kv,)),
+            dma, dma,
         ],
         compiler_params=pltpu.CompilerParams(
             collective_id=0, has_side_effects=True, vmem_limit_bytes=66977792

time: 22.3 us -> 20.9 us (0.937)
  the two profiles are of different devices: /device:TPU:1 before, /device:TPU:0 now
where the time goes in v3:
time: 20.9 us; the launch traced here: 20.7 us
  Pallas kernels  20.1 us (96%)
  local copies, waits for them, and re-layouts  0.63 us (3%)
    pallas_call x1, Pallas kernels, on_device(): pl.pallas_call(functools.partial(kernel, n), out_shape=pltpu.VMEM(queries...  20.1 us
    unnamed x1, local copies, waits for them, and re-layouts  0.63 us

profile of v3, /device:TPU:0, one launch (start us, length us, event | category | flops | bytes accessed | tf_op | source)
XLA Modules:
  0.0 20.7 jit_solution(4039955811397954946)
XLA Ops:
  0.0 20.1 %paged.1 = bf16[8,32,128]{2,1,0:T(8,128)(2,1)S(1)} custom-call(s32[8]{0:T(128)} %lens_hbm.1, bf16[8,32,128]{2,1,0:T(8,128)(2,1)} %q_hbm.1, s32[8,128]{1,0:T(8,128)} %owner_hbm.1, s32[8,128]{1,0:T(8,128)} %slot_hbm.1, bf16[64,4,128,128]{3,2,1,0:T(8,128)(2,1)} %k_hbm.1, bf16[64,4,128,128]{3,2,1,0:T(8,128)(2,1)} %v_hbm.1), custom_call_target="tpu_custom_call" | custom-call | tf_op jit(solution)/shard_map/paged/pallas_call | solution.py:331
  20.1 0.6 %copy.8 = bf16[8,32,128]{2,1,0:T(8,128)(2,1)} copy(bf16[8,32,128]{2,1,0:T(8,128)(2,1)S(1)} %paged.1) | data formatting | bytes 131072

commit v4 on v3

--- a/solution.py
+++ b/solution.py
@@ -10,7 +10,7 @@
 
 MASKED = -1e30
 CODE = 256.0
-LATE = 0
+LATE = 1
 DEPTH = 3
 F32 = jnp.float32
 BF16 = jnp.bfloat16
@@ -198,7 +198,6 @@
     tops = [jnp.full((group, 128), MASKED, F32) for _ in range(kv)]
     sums = [jnp.zeros((group, 128), F32) for _ in range(kv)]
     ocopies = {}
-    scopies = {}
 
     def gather(h):
         landed(qall.at[h, pl.ds(block, (n - 1) * block)], qrs.at[h])
@@ -242,27 +241,32 @@
             axis=0,
         ).astype(BF16)
 
-    def statistics():
+    wide = 2 * rows
+    place = lane // wide == -iota((group, 128), 0) % (128 // wide)
+
+    def shifted(x, by):
+        return pltpu.roll(x, by % 128, 1) if by % 128 else x
+
+    def statistics(h):
         for off in range(n):
-            stat = jnp.zeros((group, 128), F32)
-            for g in range(kv):
-                for j, x in enumerate((tops[g], sums[g])):
-                    at = (2 * g + j) * rows
-                    shift = (at - off * rows) % 128
-                    y = pltpu.roll(x, shift, 1) if shift else x
-                    stat = jnp.where((lane >= at) & (lane < at + rows), y, stat)
+            stat = jnp.where(lane < rows, shifted(tops[h], -off * rows), 0.0)
+            total = shifted(sums[h], (1 - off) * rows)
+            stat = jnp.where((lane >= rows) & (lane < wide), total, stat)
+            by = wide
+            while by < 128:
+                stat = stat + shifted(stat, by)
+                by *= 2
+            stat = jnp.sum(jnp.where(place, stat, 0.0), axis=0, keepdims=True)
             if off == 0:
-                srecv[0] = stat
+                srecv[h, 0] = stat
             else:
-                ssend[off] = stat
-                scopies[off] = remote(
-                    ssend.at[off], srecv.at[off], sss, srs, source(off)
-                )
-                scopies[off].start()
+                ssend[h, off] = stat
+                remote(
+                    ssend.at[h, off], srecv.at[h, off], sss, srs.at[h], source(off)
+                ).start()
 
     def finish(h):
-        if h == kv - 1:
-            statistics()
+        statistics(h)
         osend[h] = jnp.dot(m[...], ohi[...], preferred_element_type=F32).astype(BF16)
         for off in range(1, n):
             ocopies[h, off] = remote(
@@ -287,36 +291,36 @@
             if i == pairs - 1:
                 finish(h)
 
-    landed(srecv.at[pl.ds(1, n - 1)], srs)
-    stats = [srecv[off] for off in range(n)]
-    best = functools.reduce(jnp.maximum, stats)
-    factors = [jnp.exp2(x - best) for x in stats]
-    whole = functools.reduce(
-        jnp.add, [f * pltpu.roll(x, 128 - rows, 1) for f, x in zip(factors, stats)]
-    )
-    factors = [f / whole for f in factors]
-    parts = []
-    for h in range(kv):
+    for h in range(kv):
+        landed(srecv.at[h, pl.ds(1, n - 1)], srs.at[h])
+        stats = [
+            pltpu.roll(
+                jnp.broadcast_to(srecv[h, off], (group, 128)),
+                0, 1, stride=wide, stride_axis=0,
+            )
+            for off in range(n)
+        ]
+        best = functools.reduce(jnp.maximum, stats)
+        factors = [jnp.exp2(x - best) for x in stats]
+        whole = functools.reduce(
+            jnp.add, [f * pltpu.roll(x, 128 - rows, 1) for f, x in zip(factors, stats)]
+        )
+        factors = [f / whole for f in factors]
         landed(orecv.at[h, pl.ds(1, n - 1)], ors.at[h])
         gathered = []
         for off in range(n):
             got = orecv[h, off] if off else osend[h, 0:block, :]
             gathered.append(got.astype(F32).reshape(rows, group, width))
-        per_row = []
         for r in range(rows):
-            at = 2 * h * rows + r
-            total = factors[0][:, at : at + 1] * gathered[0][r]
+            total = factors[0][:, r : r + 1] * gathered[0][r]
             for off in range(1, n):
-                total = total + factors[off][:, at : at + 1] * gathered[off][r]
-            per_row.append(total)
-        parts.append(per_row)
-    for r in range(rows):
-        out_ref[r] = jnp.concatenate([parts[h][r] for h in range(kv)], axis=0).astype(BF16)
+                total = total + factors[off][:, r : r + 1] * gathered[off][r]
+            out_ref[r, h * group : (h + 1) * group, :] = total.astype(BF16)
 
     sent(trecv.at[pl.ds(1, n - 1)], tss)
     sent(qall.at[:, pl.ds(block, (n - 1) * block)], qss)
     sent(osend.at[:, pl.ds(block, (n - 1) * block)], oss)
-    sent(srecv.at[pl.ds(1, n - 1)], sss)
+    sent(srecv.at[:, pl.ds(1, n - 1)], sss)
 
 
 def on_device(n, queries, page_owner, page_slot, lengths, keys, values):
@@ -352,13 +356,13 @@
             pltpu.VMEM((pg, width), BF16),
             pltpu.VMEM((kv, n * block, width), BF16),
             pltpu.VMEM((kv, n, block, width), BF16),
-            pltpu.VMEM((n, group, 128), F32),
-            pltpu.VMEM((n, group, 128), F32),
+            pltpu.VMEM((kv, n, 1, 128), F32),
+            pltpu.VMEM((kv, n, 1, 128), F32),
             dma((4,)), dma((kv,)), dma((kv,)),
             dma, dma,
             dma, dma((kv,)),
             dma, dma((kv,)),
-            dma, dma,
+            dma, dma((kv,)),
         ],
         compiler_params=pltpu.CompilerParams(
             collective_id=0, has_side_effects=True, vmem_limit_bytes=66977792

time: 20.9 us -> 20.3 us (0.971)
  Pallas kernels: 20.1 us -> 19.5 us
    pallas_call x1, Pallas kernels: 20.1 us -> 19.5 us  [on_device(): pl.pallas_call(functools.partial(kernel, n), out_shape=pltpu.VMEM(queries...]
where the time goes in v4:
time: 20.3 us; the launch traced here: 20.1 us
  Pallas kernels  19.5 us (96%)
  local copies, waits for them, and re-layouts  0.63 us (3%)
    pallas_call x1, Pallas kernels, on_device(): pl.pallas_call(functools.partial(kernel, n), out_shape=pltpu.VMEM(queries...  19.5 us
    unnamed x1, local copies, waits for them, and re-layouts  0.63 us

profile of v4, /device:TPU:0, one launch (start us, length us, event | category | flops | bytes accessed | tf_op | source)
XLA Modules:
  0.0 20.1 jit_solution(13920545284875050590)
XLA Ops:
  0.0 19.5 %paged.1 = bf16[8,32,128]{2,1,0:T(8,128)(2,1)S(1)} custom-call(s32[8]{0:T(128)} %lens_hbm.1, bf16[8,32,128]{2,1,0:T(8,128)(2,1)} %q_hbm.1, s32[8,128]{1,0:T(8,128)} %owner_hbm.1, s32[8,128]{1,0:T(8,128)} %slot_hbm.1, bf16[64,4,128,128]{3,2,1,0:T(8,128)(2,1)} %k_hbm.1, bf16[64,4,128,128]{3,2,1,0:T(8,128)(2,1)} %v_hbm.1), custom_call_target="tpu_custom_call" | custom-call | tf_op jit(solution)/shard_map/paged/pallas_call | solution.py:335
  19.5 0.6 %copy.8 = bf16[8,32,128]{2,1,0:T(8,128)(2,1)} copy(bf16[8,32,128]{2,1,0:T(8,128)(2,1)S(1)} %paged.1) | data formatting | bytes 131072
